TPU v7x, 256 devices: a whole 4x4x8 slice. The times are simulated.
256 devices in a mesh: section: 8 (over z), rep: 32 (over x, y, core).
Axes of the slice: x: 4, y: 4, z: 8, core: 2. Of those that a mesh axis runs over, the one named last changes fastest.
Arguments:
- tokens: bfloat16 [4, 4096, 1024], P(None, 'rep'), may hold values from -6 to 6
- replica_of_row: int32 [4, 4096, 1], P(None, 'rep'), may hold values from 0 to 63; in each aligned block of 128 rows (0 to 127, 128 to 255, ..., all dimensions but the last counted through in order) at most 3 rows name the same one
- widths: int32 [64], replicated, may hold values from 512 to 1024, as said below
- placement: int32 [64], replicated, may hold values from 0 to 95, as said below
- gains: float32 [8, 96, 1024], P('section', 'rep'), may hold values from 0.5 to 1.5
- weights: bfloat16 [8, 96, 1024, 1024], P('section', 'rep'), may hold values from -0.1875 to 0.1875
Outputs:
- final: bfloat16 [4, 4096, 1024], P(None, 'rep', 'section')
Inputs may be any that keep to these rules, and one draw needn't show every extreme that they name: `widths`: multiples of 128 from 512 to 1024. `placement`: distinct slots; slot g lies on index g // 3 of rep. `replica_of_row`: within the 128 tokens of one index of rep in one micro-batch, no replica is named by more than 3 tokens.
All inputs are finite; a program needn't handle non-finite values.
Results may differ from a plain program's by a relative error of at most 0.008.
Values may be sent and summed in bfloat16 or wider, within the bound.
A program may use at most 64 MiB of HBM per device.

v0:
```python
import jax
import jax.numpy as jnp
from jax import lax
from jax.sharding import Mesh
from jax.sharding import PartitionSpec as P

REP = ("rep_0", "rep_1", "rep_2")


epsilon = 1e-05


def in_blocks(x, dim, length):
    dims = x.shape
    blocks = x.reshape(*dims[:dim], length, dims[dim] // length, *dims[dim + 1 :])
    return jnp.moveaxis(blocks, dim, 0)


def laid_out(blocks, dim):
    dims = list(blocks.shape[1:])
    dims[dim] *= blocks.shape[0]
    return jnp.moveaxis(blocks, 0, dim).reshape(dims)


def exchange_in_order(blocks, axes, sequence):
    inside = blocks.shape[1:]
    result = blocks.reshape(*(lax.axis_size(a) for a in axes), *inside)
    for k in sequence:
        result = lax.all_to_all(result, axes[k], k, k, tiled=True)
    return result.reshape(-1, *inside)


def exchange_by_chip(x, groups, sequence, split_dim, concat_dim):
    length = lax.axis_size(groups[0]) * lax.axis_size(groups[1])
    blocks = in_blocks(x, split_dim, length)
    return laid_out(exchange_in_order(blocks, groups, sequence), concat_dim)


def shifted(x, axis, by):
    length = lax.axis_size(axis)
    pairs = [(i, i + by) for i in range(length) if 0 <= i + by < length]
    return lax.ppermute(x, axis, pairs)


def summed_on_arrival(x, axis, dim):
    length = lax.axis_size(axis)
    blocks = lax.all_to_all(in_blocks(x, dim, length), axis, 0, 0, tiled=True)
    return jnp.sum(blocks.astype(jnp.float32), axis=0)


def on_device(tokens, replica_of_row, widths, placement, gains, weights):
    batches, row_count, width_max = tokens.shape
    rep_count = lax.axis_size(REP)
    section_count = lax.axis_size("section")
    slot_count = weights.shape[1]
    replica_count = widths.shape[0]
    total_slots = slot_count * rep_count
    capacity = (3 * row_count + 2 * replica_count - 1) // (2 * replica_count)
    section_id = lax.axis_index("section")
    rep_id = lax.axis_index(REP)
    final_section = section_count - 1
    features = jnp.arange(width_max, dtype=jnp.int32)
    replica_ids = jnp.arange(replica_count, dtype=jnp.int32)
    global_ids = rep_id * slot_count + jnp.arange(slot_count, dtype=jnp.int32)
    slot_width = jnp.sum(
        (placement[None, :] == global_ids[:, None]).astype(jnp.int32) * widths[None, :], axis=1
    )
    slot_live = (features[None, :] < slot_width[:, None]).astype(jnp.float32)
    slot_scale = 1.0 / jnp.maximum(slot_width, 1).astype(jnp.float32)
    section_gain = gains[0]
    section_weight = weights[0]
    slot_targets = jnp.arange(total_slots * capacity, dtype=jnp.int32)
    slot_numbers = jnp.arange(total_slots, dtype=jnp.int32)

    def routing(row_replica):
        picked = (row_replica[:, None] == replica_ids[None, :]).astype(jnp.int32)
        slot_of_row = jnp.sum(picked * placement[None, :], axis=1)
        row_width = jnp.sum(picked * widths[None, :], axis=1)
        slot_hits = (slot_of_row[:, None] == slot_numbers[None, :]).astype(jnp.int32)
        earlier = jnp.cumsum(slot_hits, axis=0) - slot_hits
        position = jnp.sum(earlier * slot_hits, axis=1)
        target = slot_of_row * capacity + position
        routing_table = (slot_targets[:, None] == target[None, :]).astype(jnp.bfloat16)
        return (routing_table, row_width)

    def update(buffer):
        float_rows = buffer.astype(jnp.float32)
        mean_square = jnp.sum(float_rows * float_rows, axis=-1) * slot_scale[None, :, None]
        lowered = (
            float_rows
            * lax.rsqrt(mean_square + epsilon)[..., None]
            * section_gain[None, :, None, :]
        ).astype(jnp.bfloat16)
        projected = jnp.einsum(
            "nscd,sde->nsce", lowered, section_weight, preferred_element_type=jnp.float32
        )
        return (float_rows + jax.nn.silu(projected) * slot_live[None, :, None, :]).astype(
            jnp.bfloat16
        )

    def unchanged(buffer):
        return buffer

    tick_count = batches + section_count - 1
    routing_tables, row_widths = jax.vmap(routing)(replica_of_row[:, :, 0])
    entering = jnp.where(
        features[None, None, :] < row_widths[:, :, None], tokens, jnp.zeros((), jnp.bfloat16)
    )
    outgoing = jnp.einsum(
        "mgr,mrd->mgd", routing_tables, entering, preferred_element_type=jnp.float32
    ).astype(jnp.bfloat16)
    outgoing = outgoing.reshape(batches, rep_count, slot_count * capacity, width_max)
    arrived_all = exchange_by_chip(outgoing, (("rep_0", "rep_1"), "rep_2"), (1, 0), 1, 1)
    arrived_all = arrived_all.reshape(batches, rep_count, slot_count, capacity, width_max)

    def tick(counter, carry):
        incoming, outbuf = carry
        index = counter - section_id
        valid = (index >= 0) & (index < batches)
        clipped = jnp.clip(index, 0, batches - 1)
        first_input = lax.dynamic_index_in_dim(arrived_all, clipped, 0, keepdims=False)
        current = jnp.where(section_id == 0, first_input, incoming)
        updated = lax.cond(valid, update, unchanged, current)
        storing = valid & (section_id == final_section)
        stored = lax.dynamic_update_index_in_dim(outbuf, updated, clipped, 0)
        outbuf = jnp.where(storing, stored, outbuf)
        incoming = shifted(updated, "section", 1)
        return (incoming, outbuf)

    start_slots = jnp.zeros((rep_count, slot_count, capacity, width_max), jnp.bfloat16)
    start_out = jnp.zeros((batches, rep_count, slot_count, capacity, width_max), jnp.bfloat16)
    last_slots, slot_results = lax.fori_loop(0, tick_count, tick, (start_slots, start_out))
    returned = lax.all_to_all(
        slot_results.reshape(batches, rep_count, slot_count * capacity, width_max),
        REP,
        split_axis=1,
        concat_axis=1,
        tiled=True,
    )
    flat_back = returned.reshape(batches, total_slots * capacity, width_max)
    final_rows = jnp.einsum(
        "mgr,mgd->mrd", routing_tables, flat_back, preferred_element_type=jnp.float32
    ).astype(jnp.bfloat16)
    contribution = jnp.where(
        section_id == final_section, final_rows.astype(jnp.float32), jnp.zeros((), jnp.float32)
    )
    gathered = summed_on_arrival(contribution.astype(jnp.bfloat16), "section", 2)
    return gathered.astype(jnp.bfloat16)


def solution(mesh):
    torus = Mesh(
        mesh.devices.reshape(mesh.shape["section"], 4, 4, 2), ("section", "rep_0", "rep_1", "rep_2")
    )
    in_specs = (
        P(None, REP, None),
        P(None, REP, None),
        P(),
        P(),
        P("section", REP, None),
        P("section", REP, None, None),
    )
    out_specs = P(None, REP, "section")
    return jax.shard_map(
        on_device, mesh=torus, in_specs=in_specs, out_specs=out_specs, check_vma=False
    )
```

profile of v0, /device:TPU:1, one launch (start us, length us, event | category | flops | bytes accessed | tf_op | source)
XLA Modules:
  0.0 354.8 jit_solution(17011968048559300156)
XLA Ops:
  6.9 8.5 %all_to_all.20 = bf16[16,2,4,1,9,1024]{5,2,4,0,3,1:T(4,128)(2,1)S(1)} all-to-all(bf16[16,2,4,1,9,1024]{5,2,4,0,3,1:T(4,128)(2,1)S(1)} %copy.24), channel_id=1, replica_groups=mesh['section'=8,'rep_0'=4,'rep_1'=4,'rep_2'=2] {'rep_2'}, dimensions={1} | all-to-all | bytes 4718592 | tf_op jit(solution)/shard_map/all_to_all | solution.py:29
  18.0 5.2 %all-to-all-start.1 = ((bf16[16,2,4,1,9,1024]{5,2,4,1,3,0:T(4,128)(2,1)}), bf16[16,2,4,1,9,1024]{5,2,4,1,3,0:T(4,128)(2,1)S(1)}, u32[]{:S(2)}, u32[]{:S(2)}) async-start(bf16[16,2,4,1,9,1024]{5,2,4,1,3,0:T(4,128)(2,1)} %copy.25), calls=%async_computation.1 | async-start | bytes 4718592 | tf_op jit(solution)/shard_map/all_to_all | solution.py:29
  25.8 29.3 %all-to-all-done.1 = bf16[16,2,4,1,9,1024]{5,2,4,1,3,0:T(4,128)(2,1)S(1)} async-done(((bf16[16,2,4,1,9,1024]{5,2,4,1,3,0:T(4,128)(2,1)}), bf16[16,2,4,1,9,1024]{5,2,4,1,3,0:T(4,128)(2,1)S(1)}, u32[]{:S(2)}, u32[]{:S(2)}) %all-to-all-start.1) | async-done | bytes 2359328 | tf_op jit(solution)/shard_map/all_to_all | solution.py:29
  57.6 189.9 %while.17 = (s32[]{:T(128)}, bf16[32,3,3,1024]{3,0,2,1:T(8,128)(2,1)S(1)}, bf16[4,32,3,3,1024]{4,1,3,2,0:T(8,128)(2,1)S(1)}, s32[]{:T(128)}, pred[]{:T(512)}, /*...) while((s32[]{:T(128)}, ...), condition=%wide.region_9.10_spmd.clone, body=%wide.region_5.9_spmd.clone.sunk | while | flops 608999680 | bytes 15180616 | solution.py:132
  59.5 5.2 %conditional.3 = (bf16[32,3,3,1024]{3,0,2,1:T(8,128)(2,1)S(1)}) conditional(s32[]{:T(128)} %convert_element_type.90, bf16[32,3,3,1024]{3,0,2,1:T(8,128)(2,1)S(1)} %bitcast_select_fusion.3, (bf16[32,3,3,1024]{3,0,2,1:T(8,128)(2,1)S(1)}, f32[3]{0:T(128)}, f32[1,3,1024]{2,1,0:T(4,128)}, bf16[3,1024,1024]{2,1,0:T(8,128)(2,1)}, ...), branch_computations={%region_6.6_spmd, %region_7.8_spmd} | conditional | flops 608403712 | bytes 9269780 | solution.py:123
  60.4 4.2 %fusion.10 = bf16[32,3,3,1024]{3,0,2,1:T(8,128)(2,1)S(1)} fusion(bf16[32,3,3,1024]{3,0,2,1:T(8,128)(2,1)S(1)} %copy.56, bf16[3,1024,1024]{2,1,0:T(8,128)(2,1)} %get-tuple-element.218, f32[3,1024]{1,0:T(4,128)S(1)} %get-tuple-element.219, f32[3,1024]{1,0:T(4,128)} %bitcast.51, f32[32,3,3]{0,2,1:T(4,128)S(1)} %add_rsqrt_fusion), kind=kOutput, calls=%fused_computation.10 | convolution fusion | flops 607518720 | bytes 7496832 | tf_op jit(solution)/shard_map/while/body/eval_jaxpr/cond/branch_1_fun/nscd,sde->nsce/dot_general | solution.py:94
  66.3 10.2 %collective-permute-done = bf16[32,3,3,1024]{3,0,2,1:T(8,128)(2,1)S(1)} collective-permute-done((bf16[32,3,3,1024]{3,0,2,1:T(8,128)(2,1)S(1)}, bf16[32,3,3,1024]{3,0,2,1:T(8,128)(2,1)S(1)}, u32[]{:S(2)}, u32[]{:S(2)}) %collective-permute-start) | collective-permute-done | bytes 589856 | tf_op jit(solution)/shard_map/while/body/eval_jaxpr/ppermute | solution.py:42
  78.3 5.2 %conditional.3 = (bf16[32,3,3,1024]{3,0,2,1:T(8,128)(2,1)S(1)}) conditional(s32[]{:T(128)} %convert_element_type.90, bf16[32,3,3,1024]{3,0,2,1:T(8,128)(2,1)S(1)} %bitcast_select_fusion.3, (bf16[32,3,3,1024]{3,0,2,1:T(8,128)(2,1)S(1)}, f32[3]{0:T(128)}, f32[1,3,1024]{2,1,0:T(4,128)}, bf16[3,1024,1024]{2,1,0:T(8,128)(2,1)}, ...), branch_computations={%region_6.6_spmd, %region_7.8_spmd} | conditional | flops 608403712 | bytes 9269780 | solution.py:123
  79.3 4.2 %fusion.10 = bf16[32,3,3,1024]{3,0,2,1:T(8,128)(2,1)S(1)} fusion(bf16[32,3,3,1024]{3,0,2,1:T(8,128)(2,1)S(1)} %copy.56, bf16[3,1024,1024]{2,1,0:T(8,128)(2,1)} %get-tuple-element.218, f32[3,1024]{1,0:T(4,128)S(1)} %get-tuple-element.219, f32[3,1024]{1,0:T(4,128)} %bitcast.51, f32[32,3,3]{0,2,1:T(4,128)S(1)} %add_rsqrt_fusion), kind=kOutput, calls=%fused_computation.10 | convolution fusion | flops 607518720 | bytes 7496832 | tf_op jit(solution)/shard_map/while/body/eval_jaxpr/cond/branch_1_fun/nscd,sde->nsce/dot_general | solution.py:94
  83.5 4.1 %collective-permute-start = (bf16[32,3,3,1024]{3,0,2,1:T(8,128)(2,1)S(1)}, bf16[32,3,3,1024]{3,0,2,1:T(8,128)(2,1)S(1)}, u32[]{:S(2)}, u32[]{:S(2)}) collective-permute-start(bf16[32,3,3,1024]{3,0,2,1:T(8,128)(2,1)S(1)} %get-tuple-element.439), channel_id=1, source_target_pairs={{0,32},{32,64},{64,96},{96,128},{128,160},{160,192},{192,224},{1,3... | collective-permute-start | bytes 1769480 | tf_op jit(solution)/shard_map/while/body/eval_jaxpr/ppermute | solution.py:42
  87.9 9.3 %collective-permute-done = bf16[32,3,3,1024]{3,0,2,1:T(8,128)(2,1)S(1)} collective-permute-done((bf16[32,3,3,1024]{3,0,2,1:T(8,128)(2,1)S(1)}, bf16[32,3,3,1024]{3,0,2,1:T(8,128)(2,1)S(1)}, u32[]{:S(2)}, u32[]{:S(2)}) %collective-permute-start) | collective-permute-done | bytes 589856 | tf_op jit(solution)/shard_map/while/body/eval_jaxpr/ppermute | solution.py:42
  99.1 5.2 %conditional.3 = (bf16[32,3,3,1024]{3,0,2,1:T(8,128)(2,1)S(1)}) conditional(s32[]{:T(128)} %convert_element_type.90, bf16[32,3,3,1024]{3,0,2,1:T(8,128)(2,1)S(1)} %bitcast_select_fusion.3, (bf16[32,3,3,1024]{3,0,2,1:T(8,128)(2,1)S(1)}, f32[3]{0:T(128)}, f32[1,3,1024]{2,1,0:T(4,128)}, bf16[3,1024,1024]{2,1,0:T(8,128)(2,1)}, ...), branch_computations={%region_6.6_spmd, %region_7.8_spmd} | conditional | flops 608403712 | bytes 9269780 | solution.py:123
  100.0 4.2 %fusion.10 = bf16[32,3,3,1024]{3,0,2,1:T(8,128)(2,1)S(1)} fusion(bf16[32,3,3,1024]{3,0,2,1:T(8,128)(2,1)S(1)} %copy.56, bf16[3,1024,1024]{2,1,0:T(8,128)(2,1)} %get-tuple-element.218, f32[3,1024]{1,0:T(4,128)S(1)} %get-tuple-element.219, f32[3,1024]{1,0:T(4,128)} %bitcast.51, f32[32,3,3]{0,2,1:T(4,128)S(1)} %add_rsqrt_fusion), kind=kOutput, calls=%fused_computation.10 | convolution fusion | flops 607518720 | bytes 7496832 | tf_op jit(solution)/shard_map/while/body/eval_jaxpr/cond/branch_1_fun/nscd,sde->nsce/dot_general | solution.py:94
  108.7 8.5 %collective-permute-done = bf16[32,3,3,1024]{3,0,2,1:T(8,128)(2,1)S(1)} collective-permute-done((bf16[32,3,3,1024]{3,0,2,1:T(8,128)(2,1)S(1)}, bf16[32,3,3,1024]{3,0,2,1:T(8,128)(2,1)S(1)}, u32[]{:S(2)}, u32[]{:S(2)}) %collective-permute-start) | collective-permute-done | bytes 589856 | tf_op jit(solution)/shard_map/while/body/eval_jaxpr/ppermute | solution.py:42
  119.0 5.2 %conditional.3 = (bf16[32,3,3,1024]{3,0,2,1:T(8,128)(2,1)S(1)}) conditional(s32[]{:T(128)} %convert_element_type.90, bf16[32,3,3,1024]{3,0,2,1:T(8,128)(2,1)S(1)} %bitcast_select_fusion.3, (bf16[32,3,3,1024]{3,0,2,1:T(8,128)(2,1)S(1)}, f32[3]{0:T(128)}, f32[1,3,1024]{2,1,0:T(4,128)}, bf16[3,1024,1024]{2,1,0:T(8,128)(2,1)}, ...), branch_computations={%region_6.6_spmd, %region_7.8_spmd} | conditional | flops 608403712 | bytes 9269780 | solution.py:123
  120.0 4.2 %fusion.10 = bf16[32,3,3,1024]{3,0,2,1:T(8,128)(2,1)S(1)} fusion(bf16[32,3,3,1024]{3,0,2,1:T(8,128)(2,1)S(1)} %copy.56, bf16[3,1024,1024]{2,1,0:T(8,128)(2,1)} %get-tuple-element.218, f32[3,1024]{1,0:T(4,128)S(1)} %get-tuple-element.219, f32[3,1024]{1,0:T(4,128)} %bitcast.51, f32[32,3,3]{0,2,1:T(4,128)S(1)} %add_rsqrt_fusion), kind=kOutput, calls=%fused_computation.10 | convolution fusion | flops 607518720 | bytes 7496832 | tf_op jit(solution)/shard_map/while/body/eval_jaxpr/cond/branch_1_fun/nscd,sde->nsce/dot_general | solution.py:94
  128.6 7.6 %collective-permute-done = bf16[32,3,3,1024]{3,0,2,1:T(8,128)(2,1)S(1)} collective-permute-done((bf16[32,3,3,1024]{3,0,2,1:T(8,128)(2,1)S(1)}, bf16[32,3,3,1024]{3,0,2,1:T(8,128)(2,1)S(1)}, u32[]{:S(2)}, u32[]{:S(2)}) %collective-permute-start) | collective-permute-done | bytes 589856 | tf_op jit(solution)/shard_map/while/body/eval_jaxpr/ppermute | solution.py:42
  138.1 9.3 %collective-permute-start = (bf16[32,3,3,1024]{3,0,2,1:T(8,128)(2,1)S(1)}, bf16[32,3,3,1024]{3,0,2,1:T(8,128)(2,1)S(1)}, u32[]{:S(2)}, u32[]{:S(2)}) collective-permute-start(bf16[32,3,3,1024]{3,0,2,1:T(8,128)(2,1)S(1)} %get-tuple-element.439), channel_id=1, source_target_pairs={{0,32},{32,64},{64,96},{96,128},{128,160},{160,192},{192,224},{1,3... | collective-permute-start | bytes 1769480 | tf_op jit(solution)/shard_map/while/body/eval_jaxpr/ppermute | solution.py:42
  147.7 6.8 %collective-permute-done = bf16[32,3,3,1024]{3,0,2,1:T(8,128)(2,1)S(1)} collective-permute-done((bf16[32,3,3,1024]{3,0,2,1:T(8,128)(2,1)S(1)}, bf16[32,3,3,1024]{3,0,2,1:T(8,128)(2,1)S(1)}, u32[]{:S(2)}, u32[]{:S(2)}) %collective-permute-start) | collective-permute-done | bytes 589856 | tf_op jit(solution)/shard_map/while/body/eval_jaxpr/ppermute | solution.py:42
  160.8 6.5 %collective-permute-done = bf16[32,3,3,1024]{3,0,2,1:T(8,128)(2,1)S(1)} collective-permute-done((bf16[32,3,3,1024]{3,0,2,1:T(8,128)(2,1)S(1)}, bf16[32,3,3,1024]{3,0,2,1:T(8,128)(2,1)S(1)}, u32[]{:S(2)}, u32[]{:S(2)}) %collective-permute-start) | collective-permute-done | bytes 589856 | tf_op jit(solution)/shard_map/while/body/eval_jaxpr/ppermute | solution.py:42
  169.2 8.2 %collective-permute-start = (bf16[32,3,3,1024]{3,0,2,1:T(8,128)(2,1)S(1)}, bf16[32,3,3,1024]{3,0,2,1:T(8,128)(2,1)S(1)}, u32[]{:S(2)}, u32[]{:S(2)}) collective-permute-start(bf16[32,3,3,1024]{3,0,2,1:T(8,128)(2,1)S(1)} %get-tuple-element.439), channel_id=1, source_target_pairs={{0,32},{32,64},{64,96},{96,128},{128,160},{160,192},{192,224},{1,3... | collective-permute-start | bytes 1769480 | tf_op jit(solution)/shard_map/while/body/eval_jaxpr/ppermute | solution.py:42
  177.6 6.5 %collective-permute-done = bf16[32,3,3,1024]{3,0,2,1:T(8,128)(2,1)S(1)} collective-permute-done((bf16[32,3,3,1024]{3,0,2,1:T(8,128)(2,1)S(1)}, bf16[32,3,3,1024]{3,0,2,1:T(8,128)(2,1)S(1)}, u32[]{:S(2)}, u32[]{:S(2)}) %collective-permute-start) | collective-permute-done | bytes 589856 | tf_op jit(solution)/shard_map/while/body/eval_jaxpr/ppermute | solution.py:42
  186.1 4.3 %collective-permute-start = (bf16[32,3,3,1024]{3,0,2,1:T(8,128)(2,1)S(1)}, bf16[32,3,3,1024]{3,0,2,1:T(8,128)(2,1)S(1)}, u32[]{:S(2)}, u32[]{:S(2)}) collective-permute-start(bf16[32,3,3,1024]{3,0,2,1:T(8,128)(2,1)S(1)} %get-tuple-element.439), channel_id=1, source_target_pairs={{0,32},{32,64},{64,96},{96,128},{128,160},{160,192},{192,224},{1,3... | collective-permute-start | bytes 1769480 | tf_op jit(solution)/shard_map/while/body/eval_jaxpr/ppermute | solution.py:42
  190.6 7.8 %collective-permute-done = bf16[32,3,3,1024]{3,0,2,1:T(8,128)(2,1)S(1)} collective-permute-done((bf16[32,3,3,1024]{3,0,2,1:T(8,128)(2,1)S(1)}, bf16[32,3,3,1024]{3,0,2,1:T(8,128)(2,1)S(1)}, u32[]{:S(2)}, u32[]{:S(2)}) %collective-permute-start) | collective-permute-done | bytes 589856 | tf_op jit(solution)/shard_map/while/body/eval_jaxpr/ppermute | solution.py:42
  200.3 7.5 %collective-permute-start = (bf16[32,3,3,1024]{3,0,2,1:T(8,128)(2,1)S(1)}, bf16[32,3,3,1024]{3,0,2,1:T(8,128)(2,1)S(1)}, u32[]{:S(2)}, u32[]{:S(2)}) collective-permute-start(bf16[32,3,3,1024]{3,0,2,1:T(8,128)(2,1)S(1)} %get-tuple-element.439), channel_id=1, source_target_pairs={{0,32},{32,64},{64,96},{96,128},{128,160},{160,192},{192,224},{1,3... | collective-permute-start | bytes 1769480 | tf_op jit(solution)/shard_map/while/body/eval_jaxpr/ppermute | solution.py:42
  208.1 6.5 %collective-permute-done = bf16[32,3,3,1024]{3,0,2,1:T(8,128)(2,1)S(1)} collective-permute-done((bf16[32,3,3,1024]{3,0,2,1:T(8,128)(2,1)S(1)}, bf16[32,3,3,1024]{3,0,2,1:T(8,128)(2,1)S(1)}, u32[]{:S(2)}, u32[]{:S(2)}) %collective-permute-start) | collective-permute-done | bytes 589856 | tf_op jit(solution)/shard_map/while/body/eval_jaxpr/ppermute | solution.py:42
  216.5 5.4 %collective-permute-start = (bf16[32,3,3,1024]{3,0,2,1:T(8,128)(2,1)S(1)}, bf16[32,3,3,1024]{3,0,2,1:T(8,128)(2,1)S(1)}, u32[]{:S(2)}, u32[]{:S(2)}) collective-permute-start(bf16[32,3,3,1024]{3,0,2,1:T(8,128)(2,1)S(1)} %get-tuple-element.439), channel_id=1, source_target_pairs={{0,32},{32,64},{64,96},{96,128},{128,160},{160,192},{192,224},{1,3... | collective-permute-start | bytes 1769480 | tf_op jit(solution)/shard_map/while/body/eval_jaxpr/ppermute | solution.py:42
  222.2 7.5 %collective-permute-done = bf16[32,3,3,1024]{3,0,2,1:T(8,128)(2,1)S(1)} collective-permute-done((bf16[32,3,3,1024]{3,0,2,1:T(8,128)(2,1)S(1)}, bf16[32,3,3,1024]{3,0,2,1:T(8,128)(2,1)S(1)}, u32[]{:S(2)}, u32[]{:S(2)}) %collective-permute-start) | collective-permute-done | bytes 589856 | tf_op jit(solution)/shard_map/while/body/eval_jaxpr/ppermute | solution.py:42
  231.6 9.2 %collective-permute-start = (bf16[32,3,3,1024]{3,0,2,1:T(8,128)(2,1)S(1)}, bf16[32,3,3,1024]{3,0,2,1:T(8,128)(2,1)S(1)}, u32[]{:S(2)}, u32[]{:S(2)}) collective-permute-start(bf16[32,3,3,1024]{3,0,2,1:T(8,128)(2,1)S(1)} %get-tuple-element.439), channel_id=1, source_target_pairs={{0,32},{32,64},{64,96},{96,128},{128,160},{160,192},{192,224},{1,3... | collective-permute-start | bytes 1769480 | tf_op jit(solution)/shard_map/while/body/eval_jaxpr/ppermute | solution.py:42
  241.0 6.5 %collective-permute-done = bf16[32,3,3,1024]{3,0,2,1:T(8,128)(2,1)S(1)} collective-permute-done((bf16[32,3,3,1024]{3,0,2,1:T(8,128)(2,1)S(1)}, bf16[32,3,3,1024]{3,0,2,1:T(8,128)(2,1)S(1)}, u32[]{:S(2)}, u32[]{:S(2)}) %collective-permute-start) | collective-permute-done | bytes 589856 | tf_op jit(solution)/shard_map/while/body/eval_jaxpr/ppermute | solution.py:42
  249.4 54.9 %all_to_all.21 = bf16[4,32,9,1024]{3,0,2,1:T(4,128)(2,1)S(1)} all-to-all(bf16[4,32,9,1024]{3,0,2,1:T(4,128)(2,1)S(1)} %copy.28), channel_id=1, replica_groups=mesh['section'=8,'rep_0'=4,'rep_1'=4,'rep_2'=2] {'rep_0','rep_1','rep_2'}, dimensions={1} | all-to-all | bytes 4718592 | tf_op jit(solution)/shard_map/all_to_all | solution.py:133
  306.2 47.7 %all_to_all.22 = bf16[8,4,128,128]{3,2,1,0:T(8,128)(2,1)S(1)} all-to-all(bf16[8,4,128,128]{3,2,1,0:T(8,128)(2,1)S(1)} %bitcast.49), channel_id=1, replica_groups=mesh['section'=8,'rep_0'=4,'rep_1'=4,'rep_2'=2] {'section'}, dimensions={0} | all-to-all | bytes 2097152 | tf_op jit(solution)/shard_map/all_to_all | solution.py:47
  (86 shorter events, 59.8 us)
Async XLA Ops:
  1.5 0.6 copy-start.1
  18.0 5.2 %copy-start = (f32[1,3,1024]{2,0,1:T(1,128)S(1)}, f32[1,3,1024]{2,0,1:T(1,128)}, u32[]{:S(2)}) copy-start(f32[1,3,1024]{2,0,1:T(1,128)} %param.14) | copy-start | bytes 36868
  18.0 5.8 %copy-start.3 = (s32[64]{0:T(128)S(1)}, s32[64]{0:T(128)}, u32[]{:S(2)}) copy-start(s32[64]{0:T(128)} %param.13) | copy-start | bytes 772
  18.0 5.8 %copy-start.4 = (s32[64]{0:T(128)S(1)}, s32[64]{0:T(128)}, u32[]{:S(2)}) copy-start(s32[64]{0:T(128)} %param.12) | copy-start | bytes 772
  18.0 37.1 %all-to-all-start.1 = ((bf16[16,2,4,1,9,1024]{5,2,4,1,3,0:T(4,128)(2,1)}), bf16[16,2,4,1,9,1024]{5,2,4,1,3,0:T(4,128)(2,1)S(1)}, u32[]{:S(2)}, u32[]{:S(2)}) async-start(bf16[16,2,4,1,9,1024]{5,2,4,1,3,0:T(4,128)(2,1)} %copy.25), calls=%async_computation.1 | async-start | bytes 4718592 | tf_op jit(solution)/shard_map/all_to_all | solution.py:29
  64.7 11.8 %collective-permute-start = (bf16[32,3,3,1024]{3,0,2,1:T(8,128)(2,1)S(1)}, bf16[32,3,3,1024]{3,0,2,1:T(8,128)(2,1)S(1)}, u32[]{:S(2)}, u32[]{:S(2)}) collective-permute-start(bf16[32,3,3,1024]{3,0,2,1:T(8,128)(2,1)S(1)} %get-tuple-element.439), channel_id=1, source_target_pairs={{0,32},{32,64},{64,96},{96,128},{128,160},{160,192},{192,224},{1,3... | collective-permute-start | bytes 1769480 | tf_op jit(solution)/shard_map/while/body/eval_jaxpr/ppermute | solution.py:42
  83.5 13.7 %collective-permute-start = (bf16[32,3,3,1024]{3,0,2,1:T(8,128)(2,1)S(1)}, bf16[32,3,3,1024]{3,0,2,1:T(8,128)(2,1)S(1)}, u32[]{:S(2)}, u32[]{:S(2)}) collective-permute-start(bf16[32,3,3,1024]{3,0,2,1:T(8,128)(2,1)S(1)} %get-tuple-element.439), channel_id=1, source_target_pairs={{0,32},{32,64},{64,96},{96,128},{128,160},{160,192},{192,224},{1,3... | collective-permute-start | bytes 1769480 | tf_op jit(solution)/shard_map/while/body/eval_jaxpr/ppermute | solution.py:42
  104.3 12.9 %collective-permute-start = (bf16[32,3,3,1024]{3,0,2,1:T(8,128)(2,1)S(1)}, bf16[32,3,3,1024]{3,0,2,1:T(8,128)(2,1)S(1)}, u32[]{:S(2)}, u32[]{:S(2)}) collective-permute-start(bf16[32,3,3,1024]{3,0,2,1:T(8,128)(2,1)S(1)} %get-tuple-element.439), channel_id=1, source_target_pairs={{0,32},{32,64},{64,96},{96,128},{128,160},{160,192},{192,224},{1,3... | collective-permute-start | bytes 1769480 | tf_op jit(solution)/shard_map/while/body/eval_jaxpr/ppermute | solution.py:42
  124.2 12.0 %collective-permute-start = (bf16[32,3,3,1024]{3,0,2,1:T(8,128)(2,1)S(1)}, bf16[32,3,3,1024]{3,0,2,1:T(8,128)(2,1)S(1)}, u32[]{:S(2)}, u32[]{:S(2)}) collective-permute-start(bf16[32,3,3,1024]{3,0,2,1:T(8,128)(2,1)S(1)} %get-tuple-element.439), channel_id=1, source_target_pairs={{0,32},{32,64},{64,96},{96,128},{128,160},{160,192},{192,224},{1,3... | collective-permute-start | bytes 1769480 | tf_op jit(solution)/shard_map/while/body/eval_jaxpr/ppermute | solution.py:42
  138.1 16.3 %collective-permute-start = (bf16[32,3,3,1024]{3,0,2,1:T(8,128)(2,1)S(1)}, bf16[32,3,3,1024]{3,0,2,1:T(8,128)(2,1)S(1)}, u32[]{:S(2)}, u32[]{:S(2)}) collective-permute-start(bf16[32,3,3,1024]{3,0,2,1:T(8,128)(2,1)S(1)} %get-tuple-element.439), channel_id=1, source_target_pairs={{0,32},{32,64},{64,96},{96,128},{128,160},{160,192},{192,224},{1,3... | collective-permute-start | bytes 1769480 | tf_op jit(solution)/shard_map/while/body/eval_jaxpr/ppermute | solution.py:42
  156.3 10.9 %collective-permute-start = (bf16[32,3,3,1024]{3,0,2,1:T(8,128)(2,1)S(1)}, bf16[32,3,3,1024]{3,0,2,1:T(8,128)(2,1)S(1)}, u32[]{:S(2)}, u32[]{:S(2)}) collective-permute-start(bf16[32,3,3,1024]{3,0,2,1:T(8,128)(2,1)S(1)} %get-tuple-element.439), channel_id=1, source_target_pairs={{0,32},{32,64},{64,96},{96,128},{128,160},{160,192},{192,224},{1,3... | collective-permute-start | bytes 1769480 | tf_op jit(solution)/shard_map/while/body/eval_jaxpr/ppermute | solution.py:42
  169.2 15.0 %collective-permute-start = (bf16[32,3,3,1024]{3,0,2,1:T(8,128)(2,1)S(1)}, bf16[32,3,3,1024]{3,0,2,1:T(8,128)(2,1)S(1)}, u32[]{:S(2)}, u32[]{:S(2)}) collective-permute-start(bf16[32,3,3,1024]{3,0,2,1:T(8,128)(2,1)S(1)} %get-tuple-element.439), channel_id=1, source_target_pairs={{0,32},{32,64},{64,96},{96,128},{128,160},{160,192},{192,224},{1,3... | collective-permute-start | bytes 1769480 | tf_op jit(solution)/shard_map/while/body/eval_jaxpr/ppermute | solution.py:42
  186.1 12.4 %collective-permute-start = (bf16[32,3,3,1024]{3,0,2,1:T(8,128)(2,1)S(1)}, bf16[32,3,3,1024]{3,0,2,1:T(8,128)(2,1)S(1)}, u32[]{:S(2)}, u32[]{:S(2)}) collective-permute-start(bf16[32,3,3,1024]{3,0,2,1:T(8,128)(2,1)S(1)} %get-tuple-element.439), channel_id=1, source_target_pairs={{0,32},{32,64},{64,96},{96,128},{128,160},{160,192},{192,224},{1,3... | collective-permute-start | bytes 1769480 | tf_op jit(solution)/shard_map/while/body/eval_jaxpr/ppermute | solution.py:42
  200.3 14.3 %collective-permute-start = (bf16[32,3,3,1024]{3,0,2,1:T(8,128)(2,1)S(1)}, bf16[32,3,3,1024]{3,0,2,1:T(8,128)(2,1)S(1)}, u32[]{:S(2)}, u32[]{:S(2)}) collective-permute-start(bf16[32,3,3,1024]{3,0,2,1:T(8,128)(2,1)S(1)} %get-tuple-element.439), channel_id=1, source_target_pairs={{0,32},{32,64},{64,96},{96,128},{128,160},{160,192},{192,224},{1,3... | collective-permute-start | bytes 1769480 | tf_op jit(solution)/shard_map/while/body/eval_jaxpr/ppermute | solution.py:42
  216.5 13.2 %collective-permute-start = (bf16[32,3,3,1024]{3,0,2,1:T(8,128)(2,1)S(1)}, bf16[32,3,3,1024]{3,0,2,1:T(8,128)(2,1)S(1)}, u32[]{:S(2)}, u32[]{:S(2)}) collective-permute-start(bf16[32,3,3,1024]{3,0,2,1:T(8,128)(2,1)S(1)} %get-tuple-element.439), channel_id=1, source_target_pairs={{0,32},{32,64},{64,96},{96,128},{128,160},{160,192},{192,224},{1,3... | collective-permute-start | bytes 1769480 | tf_op jit(solution)/shard_map/while/body/eval_jaxpr/ppermute | solution.py:42
  231.6 16.0 %collective-permute-start = (bf16[32,3,3,1024]{3,0,2,1:T(8,128)(2,1)S(1)}, bf16[32,3,3,1024]{3,0,2,1:T(8,128)(2,1)S(1)}, u32[]{:S(2)}, u32[]{:S(2)}) collective-permute-start(bf16[32,3,3,1024]{3,0,2,1:T(8,128)(2,1)S(1)} %get-tuple-element.439), channel_id=1, source_target_pairs={{0,32},{32,64},{64,96},{96,128},{128,160},{160,192},{192,224},{1,3... | collective-permute-start | bytes 1769480 | tf_op jit(solution)/shard_map/while/body/eval_jaxpr/ppermute | solution.py:42
  249.4 54.9 %copy-start.2 = (s32[4,128]{1,0:T(4,128)S(1)}, s32[4,128]{1,0:T(4,128)}, u32[]{:S(2)}) copy-start(s32[4,128]{1,0:T(4,128)} %copy-done.1) | copy-start | bytes 6148
where the time goes:
time: 356 us; the launch traced here: 355 us
  waiting for transfers between devices  113 us (32%)
  blocking collectives  111 us (31%)
  starting transfers between devices  67 us (19%)
  other arithmetic  30.9 us (9%)
  matrix products  20.7 us (6%)
  local copies, waits for them, and re-layouts  11.3 us (3%)
    ppermute x11, waiting for transfers between devices, shifted(): return lax.ppermute(x, axis, pairs)  83.7 us
    ppermute x11, starting transfers between devices, shifted(): return lax.ppermute(x, axis, pairs)  61.9 us
    all_to_all x1, blocking collectives, on_device(): lax.all_to_all(slot_results.reshape(batches, rep_count, slot_count * capa...  54.9 us
    all_to_all x1, blocking collectives, summed_on_arrival(): blocks = lax.all_to_all(in_blocks(x, dim, length), axis, 0, 0, tiled=True)  47.7 us
    all_to_all x1, waiting for transfers between devices, exchange_in_order(): result = lax.all_to_all(result, axes[k], k, k, tiled=True)  29.3 us
    dot_general x4, matrix products, update(): jnp.einsum('nscd,sde->nsce', lowered, section_weight, preferred_element_t...  16.9 us
    select_n x11, other arithmetic, tick(): current = jnp.where(section_id == 0, first_input, incoming)  12.4 us
    all_to_all x1, blocking collectives, exchange_in_order(): result = lax.all_to_all(result, axes[k], k, k, tiled=True)  8.46 us
  transfers between devices with their start and end apart: 12, of which 12 were waited for; matrix products, arithmetic and copies ran while one was open for 1% of the time, Pallas kernels for 0%

commit v1 on v0

v1 whole, which is shorter than its diff:
```python
import functools

import jax
import jax.numpy as jnp
from jax import lax
from jax.experimental import pallas as pl
from jax.experimental.pallas import tpu as pltpu
from jax.sharding import PartitionSpec as P

MESH = pl.DeviceIdType.MESH
epsilon = 1e-05
LANES = 128
CHUNK = 32
GROUPS = 6


def relay_kernel(
    n,
    slots,
    x_ref,
    w_ref,
    gain_ref,
    live_ref,
    scale_ref,
    out_ref,
    land,
    done,
    weights,
    final,
    w_sem,
    gather_send,
    gather_recv,
    relay_send,
    relay_recv,
    final_send,
    final_recv,
):
    me = lax.axis_index("section")
    last = n - 1
    rows = x_ref.shape[0]
    chunks = rows // CHUNK
    per_slot = chunks // slots
    span = rows // GROUPS
    per_group = chunks // GROUPS

    for s in range(slots):
        pltpu.make_async_copy(w_ref.at[s], weights.at[s], w_sem.at[s]).start()

    barrier = pltpu.get_barrier_semaphore()
    for k in range(1, n):
        pl.semaphore_signal(
            barrier, inc=1, device_id={"section": lax.rem(me + k, n)}, device_id_type=MESH
        )
    pl.semaphore_wait(barrier, n - 1)

    my_columns = pl.ds(pl.multiple_of(me * LANES, LANES), LANES)

    @pl.when(me != 0)
    def _():
        for g in range(GROUPS):
            part = pl.ds(g * span, span)
            pltpu.make_async_remote_copy(
                src_ref=x_ref.at[part],
                dst_ref=land.at[part, my_columns],
                send_sem=gather_send,
                recv_sem=gather_recv.at[g],
                device_id={"section": 0},
                device_id_type=MESH,
            ).start()

    @pl.when(me == 0)
    def _():
        land[:, :LANES] = x_ref[...]

    def here(c):
        return pl.ds(pl.multiple_of(c * CHUNK, CHUNK), CHUNK)

    def forward(c):
        return pltpu.make_async_remote_copy(
            src_ref=done.at[here(c)],
            dst_ref=land.at[here(c)],
            send_sem=relay_send.at[c],
            recv_sem=relay_recv.at[c],
            device_id={"section": lax.rem(me + 1, n)},
            device_id_type=MESH,
        )

    def spread(c, section):
        columns = pl.ds(section * LANES, LANES)
        return pltpu.make_async_remote_copy(
            src_ref=done.at[here(c), columns],
            dst_ref=final.at[here(c)],
            send_sem=final_send.at[c],
            recv_sem=final_recv.at[c],
            device_id={"section": section},
            device_id_type=MESH,
        )

    def step(c, carry):
        @pl.when((me == 0) & (lax.rem(c, per_group) == 0))
        def _():
            g = c // per_group
            part = pl.ds(pl.multiple_of(g * span, span), span)
            others = land.at[part, LANES:]
            pltpu.make_async_copy(others, others, gather_recv.at[g]).wait()

        @pl.when(me != 0)
        def _():
            forward(c).wait_recv()

        slot = c // per_slot

        @pl.when(lax.rem(c, per_slot) == 0)
        def _():
            pltpu.make_async_copy(w_ref.at[slot], weights.at[slot], w_sem.at[slot]).wait()

        hidden = land[here(c), :].astype(jnp.float32)
        mean_square = jnp.sum(hidden * hidden, axis=1, keepdims=True) * scale_ref[slot][:, :1]
        lowered = (hidden * lax.rsqrt(mean_square + epsilon) * gain_ref[slot]).astype(jnp.bfloat16)
        projected = jnp.dot(lowered, weights[slot], preferred_element_type=jnp.float32)
        done[here(c), :] = (
            hidden + projected / (1.0 + jnp.exp(-projected)) * live_ref[slot]
        ).astype(jnp.bfloat16)

        @pl.when(me != last)
        def _():
            forward(c).start()

        @pl.when(me == last)
        def _():
            for section in range(n - 1):
                spread(c, section).start()

        return carry

    lax.fori_loop(0, chunks, step, 0)

    @pl.when(me == last)
    def _():
        out_ref[...] = done[:, last * LANES :]

        def settle(c, carry):
            sent = done.at[here(c), LANES:]
            pltpu.make_async_copy(sent, sent, final_send.at[c]).wait()
            return carry

        lax.fori_loop(0, chunks, settle, 0)

    @pl.when(me != last)
    def _():
        def settle(c, carry):
            forward(c).wait_send()
            spread(c, 0).wait_recv()
            return carry

        lax.fori_loop(0, chunks, settle, 0)
        out_ref[...] = final[...]

    @pl.when(me != 0)
    def _():
        pltpu.make_async_copy(x_ref, x_ref, gather_send).wait()


def on_device(tokens, replica_of_row, widths, placement, gains, weights):
    batches, row_count, width_max = tokens.shape
    n = lax.axis_size("section")
    rep_count = lax.axis_size("rep")
    slots = weights.shape[1]
    section_id = lax.axis_index("section")
    rep_id = lax.axis_index("rep")
    tokens_all = batches * row_count
    capacity = 3
    per_pair = slots * batches * capacity
    rows = rep_count * per_pair

    row_replica = replica_of_row[:, :, 0]
    picked = row_replica[:, :, None] == jnp.arange(widths.shape[0], dtype=jnp.int32)
    slot_of_row = jnp.sum(jnp.where(picked, placement, 0), axis=2)
    row_width = jnp.sum(jnp.where(picked, widths, 0), axis=2)
    numbers = jnp.arange(row_count, dtype=jnp.int32)
    same = (row_replica[:, :, None] == row_replica[:, None, :]) & (
        numbers[None, :] < numbers[:, None]
    )
    position = jnp.sum(same.astype(jnp.int32), axis=2)
    batch = jnp.arange(batches, dtype=jnp.int32)[:, None]
    target = (slot_of_row * (batches * capacity) + batch * capacity + position).reshape(tokens_all)

    mine = lax.dynamic_slice_in_dim(tokens, section_id * LANES, LANES, axis=2)
    features = section_id * LANES + jnp.arange(LANES, dtype=jnp.int32)
    entering = jnp.where(
        features < row_width[:, :, None], mine, jnp.zeros((), jnp.bfloat16)
    ).reshape(tokens_all, LANES)
    table = (jnp.arange(rows, dtype=jnp.int32)[:, None] == target[None, :]).astype(jnp.bfloat16)
    outgoing = jnp.dot(table, entering, preferred_element_type=jnp.float32).astype(jnp.bfloat16)
    arrived = lax.all_to_all(
        outgoing.reshape(rep_count, per_pair, LANES), "rep", 0, 0, tiled=True
    )
    dense = arrived.reshape(rep_count, slots, batches * capacity, LANES)
    dense = jnp.swapaxes(dense, 0, 1).reshape(rows, LANES)

    slot_ids = rep_id * slots + jnp.arange(slots, dtype=jnp.int32)
    slot_width = jnp.sum(jnp.where(placement[None, :] == slot_ids[:, None], widths, 0), axis=1)
    live = (jnp.arange(width_max, dtype=jnp.int32) < slot_width[:, None]).astype(jnp.float32)
    scale = 1.0 / jnp.maximum(slot_width, 1).astype(jnp.float32)
    scale = jnp.broadcast_to(scale[:, None, None], (slots, 1, LANES))

    chunks = rows // CHUNK
    vmem = pl.BlockSpec(memory_space=pltpu.VMEM)
    result = pl.pallas_call(
        functools.partial(relay_kernel, n, slots),
        out_shape=jax.ShapeDtypeStruct((rows, LANES), jnp.bfloat16),
        in_specs=[vmem, pl.BlockSpec(memory_space=pl.ANY), vmem, vmem, vmem],
        out_specs=vmem,
        scratch_shapes=[
            pltpu.VMEM((rows, width_max), jnp.bfloat16),
            pltpu.VMEM((rows, width_max), jnp.bfloat16),
            pltpu.VMEM((slots, width_max, width_max), jnp.bfloat16),
            pltpu.VMEM((rows, LANES), jnp.bfloat16),
            pltpu.SemaphoreType.DMA((slots,)),
            pltpu.SemaphoreType.DMA,
            pltpu.SemaphoreType.DMA((GROUPS,)),
            pltpu.SemaphoreType.DMA((chunks,)),
            pltpu.SemaphoreType.DMA((chunks,)),
            pltpu.SemaphoreType.DMA((chunks,)),
            pltpu.SemaphoreType.DMA((chunks,)),
        ],
        compiler_params=pltpu.CompilerParams(
            collective_id=0, has_side_effects=True, vmem_limit_bytes=40 * 1024 * 1024
        ),
        name="relay",
    )(dense, weights[0], gains[0][:, None, :], live[:, None, :], scale)

    back = jnp.swapaxes(result.reshape(slots, rep_count, batches * capacity, LANES), 0, 1)
    back = lax.all_to_all(
        back.reshape(rep_count, per_pair, LANES), "rep", 0, 0, tiled=True
    ).reshape(rows, LANES)
    final = lax.dot_general(
        table, back, (((0,), (0,)), ((), ())), preferred_element_type=jnp.float32
    ).astype(jnp.bfloat16)
    return final.reshape(batches, row_count, LANES)


def solution(mesh):
    in_specs = (
        P(None, "rep", None),
        P(None, "rep", None),
        P(),
        P(),
        P("section", "rep", None),
        P("section", "rep", None, None),
    )
    return jax.shard_map(
        on_device,
        mesh=mesh,
        in_specs=in_specs,
        out_specs=P(None, "rep", "section"),
        check_vma=False,
    )
```

time: 356 us -> 159 us (0.45)
  Pallas kernels: 0 us -> 114 us
  waiting for transfers between devices: 113 us -> 9.32 us
  blocking collectives: 111 us -> 17.6 us
  starting transfers between devices: 67 us -> 8.58 us
  other arithmetic: 30.9 us -> 3.19 us
  matrix products: 20.7 us -> 1.97 us
  local copies, waits for them, and re-layouts: 11.3 us -> 4.2 us
    pallas_call x0 -> x1, Pallas kernels: none -> 114 us  [on_device(): pl.pallas_call(functools.partial(relay_kernel, n, slots), out_shape=jax.S...]
    all_to_all x3 -> x1, blocking collectives: 111 us -> 17.6 us  [on_device(): lax.all_to_all(back.reshape(rep_count, per_pair, LANES), 'rep', 0, 0, til...]
    ppermute x11 -> x0, waiting for transfers between devices: 83.7 us -> none  [shifted(): return lax.ppermute(x, axis, pairs)]
    ppermute x11 -> x0, starting transfers between devices: 61.9 us -> none  [shifted(): return lax.ppermute(x, axis, pairs)]
    all_to_all x1, waiting for transfers between devices: 29.3 us -> 9.32 us  [on_device(): lax.all_to_all(outgoing.reshape(rep_count, per_pair, LANES), 'rep', 0, 0,...]
    dot_general x6 -> x2, matrix products: 20.7 us -> 1.97 us  [the longest x1 1.46 us: on_device(): lax.dot_general(table, back, (((0,), (0,)), ((), ())), preferred_element_...]
    select_n x22 -> x1, other arithmetic: 15.1 us -> 1.04 us  [on_device(): jnp.where(features < row_width[:, :, None], mine, jnp.zeros((), jnp.bfloa...]
    convert_element_type x12 -> x1, other arithmetic: 8.32 us -> 0.08 us  [on_device(): (jnp.arange(width_max, dtype=jnp.int32) < slot_width[:, None]).astype(jnp...]
  transfers between devices with their start and end apart: 12 -> 1, of which waited for: 12 -> 1; matrix products, arithmetic and copies ran while one was open for 1% -> 0% of each run, Pallas kernels for 0% -> 0%
where the time goes in v1:
time: 159 us
  Pallas kernels  114 us (72%)
  blocking collectives  17.6 us (11%)
  waiting for transfers between devices  9.32 us (6%)
  starting transfers between devices  8.58 us (5%)
  local copies, waits for them, and re-layouts  4.2 us (3%)
  other arithmetic  3.19 us (2%)
  matrix products  1.97 us (1%)
    pallas_call x1, Pallas kernels, on_device(): pl.pallas_call(functools.partial(relay_kernel, n, slots), out_shape=jax.S...  114 us
    all_to_all x1, blocking collectives, on_device(): lax.all_to_all(back.reshape(rep_count, per_pair, LANES), 'rep', 0, 0, til...  17.6 us
    all_to_all x1, waiting for transfers between devices, on_device(): lax.all_to_all(outgoing.reshape(rep_count, per_pair, LANES), 'rep', 0, 0,...  9.32 us
    all_to_all x1, starting transfers between devices, on_device(): lax.all_to_all(outgoing.reshape(rep_count, per_pair, LANES), 'rep', 0, 0,...  8.58 us
  transfers between devices with their start and end apart: 1, of which 1 were waited for; matrix products, arithmetic and copies ran while one was open for 0% of the time, Pallas kernels for 0%

profile of v1, /device:TPU:1, one launch (start us, length us, event | category | flops | bytes accessed | tf_op | source)
XLA Modules:
  0.0 159.0 jit_solution(3446735182869231537)
XLA Ops:
  0.0 0.0 copy-start.3
  0.0 0.0 copy-start.2
  0.0 0.0 copy-start.1
  0.1 1.0 convert_reduce_fusion
  1.1 0.8 select_reduce_fusion.1
  1.9 0.1 add_bitcast_fusion
  1.9 1.0 compare_select_fusion
  3.0 0.5 convolution_convert_fusion
  3.5 0.8 reshape.111
  4.3 8.6 %all-to-all-start = ((bf16[32,36,128]{2,1,0:T(8,128)(2,1)}), bf16[32,36,128]{2,1,0:T(8,128)(2,1)S(1)}, u32[]{:S(2)}, u32[]{:S(2)}) async-start(bf16[32,36,128]{2,1,0:T(8,128)(2,1)} %reshape.111), calls=%async_computation | async-start | bytes 655360 | tf_op jit(solution)/shard_map/all_to_all | solution.py:195
  12.9 0.0 copy-done.3
  12.9 0.0 copy-done.2
  12.9 0.2 select_reduce_fusion.2
  13.1 0.1 compare_convert_fusion.live_ref
  13.1 9.3 %all-to-all-done = bf16[32,36,128]{2,1,0:T(8,128)(2,1)S(1)} async-done(((bf16[32,36,128]{2,1,0:T(8,128)(2,1)}), bf16[32,36,128]{2,1,0:T(8,128)(2,1)S(1)}, u32[]{:S(2)}, u32[]{:S(2)}) %all-to-all-start) | async-done | bytes 294944 | tf_op jit(solution)/shard_map/all_to_all | solution.py:195
  22.5 0.1 copy.16
  22.6 0.1 reshape.113.x_ref
  22.7 0.1 broadcast_in_dim.49.scale_ref
  22.8 0.0 copy-done.1
  22.8 0.0 copy-start
  22.8 2.8 %copy-done = bf16[1,3,1024,1024]{3,2,1,0:T(8,128)(2,1)S(1)} copy-done((bf16[1,3,1024,1024]{3,2,1,0:T(8,128)(2,1)S(1)}, bf16[1,3,1024,1024]{3,2,1,0:T(8,128)(2,1)}, u32[]{:S(2)}) %copy-start) | copy-done | bytes 6291480
  25.6 114.1 %relay.1 = bf16[1152,128]{1,0:T(8,128)(2,1)S(1)} custom-call(bf16[1152,128]{1,0:T(8,128)(2,1)S(1)} %reshape.113.x_ref, bf16[3,1024,1024]{2,1,0:T(8,128)(2,1)S(1)} %bitcast.14, f32[3,1,1024]{2,1,0:T(1,128)S(1)} %bitcast.15, f32[3,1,1024]{2,1,0:T(1,128)S(1)} %compare_convert_fusion.live_ref, f32[3,1,128]{2,1,0:T(1,128)S(1)} %broadcast_in_dim.49.scale_ref), custom_call_target="tpu_custom_call" | custom-call | tf_op jit(solution)/shard_map/relay/pallas_call | solution.py:209
  139.7 0.1 reshape.114
  139.7 0.1 copy.17
  139.8 0.1 copy.18
  140.0 17.6 %all_to_all.10 = bf16[32,36,128]{2,1,0:T(8,128)(2,1)S(1)} all-to-all(bf16[32,36,128]{2,1,0:T(8,128)(2,1)S(1)} %copy.18), channel_id=1, replica_groups=mesh['section'=8,'rep'=32] {'rep'}, dimensions={0} | all-to-all | bytes 589824 | tf_op jit(solution)/shard_map/all_to_all | solution.py:234
  157.5 0.1 reshape.116
  157.6 1.5 fusion.3
  (6 shorter events, 0.1 us)
Async XLA Ops:
  0.0 12.9 %copy-start.3 = (s32[64]{0:T(128)S(1)}, s32[64]{0:T(128)}, u32[]{:S(2)}) copy-start(s32[64]{0:T(128)} %param.8) | copy-start | bytes 772
  0.0 12.9 %copy-start.2 = (s32[64]{0:T(128)S(1)}, s32[64]{0:T(128)}, u32[]{:S(2)}) copy-start(s32[64]{0:T(128)} %param.9) | copy-start | bytes 772
  0.0 22.7 %copy-start.1 = (f32[1,3,1024]{2,0,1:T(1,128)S(1)}, f32[1,3,1024]{2,0,1:T(1,128)}, u32[]{:S(2)}) copy-start(f32[1,3,1024]{2,0,1:T(1,128)} %param.10) | copy-start | bytes 36868
  4.3 18.2 %all-to-all-start = ((bf16[32,36,128]{2,1,0:T(8,128)(2,1)}), bf16[32,36,128]{2,1,0:T(8,128)(2,1)S(1)}, u32[]{:S(2)}, u32[]{:S(2)}) async-start(bf16[32,36,128]{2,1,0:T(8,128)(2,1)} %reshape.111), calls=%async_computation | async-start | bytes 655360 | tf_op jit(solution)/shard_map/all_to_all | solution.py:195
  22.8 2.8 %copy-start = (bf16[1,3,1024,1024]{3,2,1,0:T(8,128)(2,1)S(1)}, bf16[1,3,1024,1024]{3,2,1,0:T(8,128)(2,1)}, u32[]{:S(2)}) copy-start(bf16[1,3,1024,1024]{3,2,1,0:T(8,128)(2,1)} %param.11) | copy-start | bytes 18874372
